TPU v7x, 32 devices: a whole 2x2x4 slice. The times are simulated.
32 devices in a mesh: bump: 4 (over y, core), nx: 2 (over x), ny: 4 (over z).
Axes of the slice: x: 2, y: 2, z: 4, core: 2. Of those that a mesh axis runs over, the one named last changes fastest.
Arguments:
- payoff: float32 [262144], P(('nx', 'ny')), may hold values from -6 to 6
- positions: float32 [262144], P(('nx', 'ny')), may hold values from -20 to 20
- tables: float32 [8, 5, 262144], P('bump', None, ('nx', 'ny')), may hold values from 0.02 to 1, as said below
- offsets: int32 [8, 1024], P(None, ('nx', 'ny')), may hold values from -1 to 1
- vol_curve: float32 [8], replicated, may hold values from 0.5 to 1.2
- bucket: int32 [64], P('bump'), may hold values from 0 to 7
- bump_size: float32 [64], P('bump'), may hold values from 0.1 to 0.4
Outputs:
- bumped_values: float32 [64, 262144], P('bump', ('nx', 'ny'))
- vega: float32 [64], P('bump')
Inputs may be any that keep to these rules, and one draw needn't show every extreme that they name: `tables`: component 0 lies in [0.9, 1], components 1 and 3 in [0.1, 0.2], components 2 and 4 in [0.02, 0.06].
All inputs are finite; a program needn't handle non-finite values.
Results may differ from a plain program's by a relative error of at most 0.0003.
Values sent between devices are 32-bit elements; how exact they have to be, the bound alone decides.
A program may use at most 64 MiB of HBM per device.

v0:
```python
import jax
import jax.numpy as jnp
from jax import lax
from jax.sharding import PartitionSpec as P


def with_halo(array, sides, width):
    for axis, dim in sides:
        peers, length = (lax.axis_size(axis), array.shape[dim])
        up = [(i, (i + 1) % peers) for i in range(peers)]
        down = [(j, i) for i, j in up]
        last = lax.slice_in_dim(array, length - width, length, axis=dim)
        initial = lax.slice_in_dim(array, 0, width, axis=dim)
        before = lax.ppermute(last, axis, up)
        after = lax.ppermute(initial, axis, down)
        array = jnp.concatenate([before, array, after], axis=dim)
    return array


def advance(padded, table, branch_nodes, variance):
    count = padded.shape[-1] - 4

    def shifted(shift_by):
        return padded[..., 2 + shift_by : 2 + shift_by + count]

    upward = table[1] + variance * table[2]
    downward = table[3] + variance * table[4]
    middle = 1.0 - upward - downward
    low_case = upward * shifted(0) + middle * shifted(-1) + downward * shifted(-2)
    even_case = upward * shifted(1) + middle * shifted(0) + downward * shifted(-1)
    high_case = upward * shifted(2) + middle * shifted(1) + downward * shifted(0)
    mixed = jnp.where(
        branch_nodes == -1, low_case, jnp.where(branch_nodes == 0, even_case, high_case)
    )
    return table[0] * mixed


def on_device(payoff, positions, tables, offsets, vol_curve, bucket, bump_size):
    step_count = vol_curve.shape[0]
    node_count = payoff.shape[0]
    block_count = offsets.shape[1]
    block_len = node_count // block_count
    step_ids = jnp.arange(step_count, dtype=jnp.int32)
    sigma_bumps = vol_curve[None, :] + bump_size[:, None] * (
        bucket[:, None] == step_ids[None, :]
    ).astype(jnp.float32)
    sigma_rows = jnp.concatenate([vol_curve[None, :], sigma_bumps], axis=0)
    variance_rows = sigma_rows * sigma_rows
    values = jnp.broadcast_to(payoff[None, :], (sigma_rows.shape[0], node_count))
    all_tables = lax.all_gather(tables, "bump", axis=0, tiled=True)
    for step in reversed(range(step_count)):
        table = all_tables[step]
        padded = with_halo(values, ((("nx", "ny"), 1),), 2)
        branch_nodes = jnp.broadcast_to(offsets[step][:, None], (block_count, block_len)).reshape(
            node_count
        )
        values = advance(padded, table, branch_nodes[None, :], variance_rows[:, step : step + 1])
    base_values = values[0]
    bumped_values = values[1:]
    partial_sums = jnp.sum(positions[None, :] * (bumped_values - base_values[None, :]), axis=1)
    totals = lax.psum(partial_sums, ("nx", "ny"))
    return (bumped_values, totals / bump_size)


def solution(mesh):
    in_specs = (
        P(("nx", "ny")),
        P(("nx", "ny")),
        P("bump", None, ("nx", "ny")),
        P(None, ("nx", "ny")),
        P(),
        P("bump"),
        P("bump"),
    )
    out_specs = (P("bump", ("nx", "ny")), P("bump"))
    return jax.shard_map(
        on_device, mesh=mesh, in_specs=in_specs, out_specs=out_specs, check_vma=False
    )
```

profile of v0, /device:TPU:0, one launch (start us, length us, event | category | flops | bytes accessed | tf_op | source)
XLA Modules:
  0.0 239.4 jit_solution(8637577802408455618)
XLA Ops:
  7.3 3.5 %copy.10 = f32[2,5,32768]{2,1,0:T(8,128)} copy(f32[2,5,32768]{2,0,1:T(2,128)} %param.9) | data formatting | bytes 2621440 | tf_op args[2]
  10.8 6.0 %collective-permute-start.1 = (f32[17,2]{1,0:T(8,128)S(1)}, f32[17,2]{1,0:T(8,128)S(1)}, u32[]{:S(2)}, u32[]{:S(2)}) collective-permute-start(f32[17,2]{1,0:T(8,128)S(1)} %broadcast_in_dim.178), channel_id=1, source_target_pairs={{1,0},{2,1},{3,2},{4,3},{5,4},{6,5},{7,6},{0,7},{9,8},{10,9},{11,1... | collective-permute-start | bytes 416 | tf_op jit(solution)/shard_map/ppermute | solution.py:15
  24.4 47.5 %all-gather.2.cloned.1.call-done = f32[8,5,32768]{2,1,0:T(8,128)} async-done(((f32[2,5,32768]{2,1,0:T(8,128)}), f32[8,5,32768]{2,1,0:T(8,128)}) %all-gather.2.cloned.1.call-update) | async-done | bytes 5242896 | tf_op jit(solution)/shard_map/all_gather | solution.py:50
  71.9 10.1 %fusion.81 = (f32[1,1,32768]{2,1,0:T(1,128)S(1)}, f32[1,1,32768]{2,1,0:T(1,128)S(1)}, f32[1,1,32768]{2,1,0:T(1,128)}, f32[1,1,32768]{2,1,0:T(1,128)}, f32[1,1,32...) fusion(f32[8,5,32768]{2,1,0:T(8,128)} %all-gather.2.cloned.1.ca, ...), kind=kLoop, calls=%fused_computation.157 | loop fusion | bytes 4980736 | tf_op jit(solution)/shard_map/slice | solution.py:26
  82.0 10.3 %fusion.80 = (f32[1,1,32768]{2,1,0:T(1,128)S(1)}, f32[1,1,32768]{2,1,0:T(1,128)S(1)}, f32[1,1,32768]{2,1,0:T(1,128)}, f32[1,1,32768]{2,1,0:T(1,128)}, f32[1,1,32...) fusion(f32[8,5,32768]{2,1,0:T(8,128)} %all-gather.2.cloned.1.ca, ...), kind=kLoop, calls=%fused_computation.156 | loop fusion | bytes 4980736 | tf_op jit(solution)/shard_map/slice | solution.py:35
  92.5 5.4 %fusion.77 = f32[17,32768]{1,0:T(8,128)S(1)} fusion(f32[17,2]{1,0:T(8,128)S(1)} %collective-permute-done.1, f32[17,32768]{1,0:T(8,128)S(1)} %broadcast_in_dim.174, f32[17,2]{1,0:T(8,128)S(1)} %collective-permute-done, f32[32768]{0:T(1024)S(1)} %bitcast.124, f32[32768]{0:T(1024)S(1)} %bitcast.125, f32[32768]{0:T(1024)S(1)} %bitcast.126, ...), kind=kLoop, calls=%fused_computation.124 | loop fusion | flops 15597568 | bytes 5177684 | tf_op jit(solution)/shard_map/mul | solution.py:35
  98.0 1.6 copy-done.2
  99.7 1.5 collective-permute-start.2
  101.1 3.2 %collective-permute-start.3 = (f32[17,2]{1,0:T(8,128)S(1)}, f32[17,2]{1,0:T(8,128)S(1)}, u32[]{:S(2)}, u32[]{:S(2)}) collective-permute-start(f32[17,2]{1,0:T(8,128)S(1)} %get-tuple-element.57), channel_id=1, source_target_pairs={{1,0},{2,1},{3,2},{4,3},{5,4},{6,5},{7,6},{0,7},{9,8},{10,9},{11,1... | collective-permute-start | bytes 416 | tf_op jit(solution)/shard_map/ppermute | solution.py:15
  105.1 0.9 collective-permute-done.2
  106.6 10.1 %fusion.69 = f32[17,32768]{1,0:T(8,128)S(1)} fusion(f32[17,2]{1,0:T(8,128)} %copy-done.12, f32[17,32768]{1,0:T(8,128)} %copy-done.2, f32[17,2]{1,0:T(8,128)S(1)} %collective-permute-done.2, f32[32768]{0:T(1024)} %bitcast.121, f32[32768]{0:T(1024)} %bitcast.122, f32[32768]{0:T(1024)} %bitcast.118, f32[17]{0:T(128)} %get-tuple-element.78, ...), kind=kLoop, calls=%fused_computation.114 | loop fusion | flops 15597568 | bytes 5177684 | tf_op jit(solution)/shard_map/mul | solution.py:35
  117.7 4.5 %collective-permute-start.5 = (f32[17,2]{1,0:T(8,128)S(1)}, f32[17,2]{1,0:T(8,128)}, u32[]{:S(2)}, u32[]{:S(2)}) collective-permute-start(f32[17,2]{1,0:T(8,128)S(1)} %get-tuple-element.55), channel_id=1, source_target_pairs={{1,0},{2,1},{3,2},{4,3},{5,4},{6,5},{7,6},{0,7},{9,8},{10,9},{11,1... | collective-permute-start | bytes 416 | tf_op jit(solution)/shard_map/ppermute | solution.py:15
  122.9 1.4 eq.270
  124.3 6.4 %fusion.61 = f32[17,32768]{1,0:T(8,128)S(1)} fusion(f32[17,2]{1,0:T(8,128)} %collective-permute-done.5, f32[17,32768]{1,0:T(8,128)S(1)} %fusion.69, f32[17,2]{1,0:T(8,128)} %collective-permute-done.4, f32[32768]{0:T(1024)} %bitcast.116, f32[32768]{0:T(1024)} %bitcast.117, f32[32768]{0:T(1024)} %bitcast.113, f32[17]{0:T(128)} %get-tuple-element.79, ...), kind=kLoop, calls=%fused_computation.104 | loop fusion | flops 15597568 | bytes 5177684 | tf_op jit(solution)/shard_map/mul | solution.py:35
  130.7 1.6 copy-done
  133.2 3.9 %collective-permute-start.7 = (f32[17,2]{1,0:T(8,128)S(1)}, f32[17,2]{1,0:T(8,128)S(1)}, u32[]{:S(2)}, u32[]{:S(2)}) collective-permute-start(f32[17,2]{1,0:T(8,128)S(1)} %get-tuple-element.53), channel_id=1, source_target_pairs={{1,0},{2,1},{3,2},{4,3},{5,4},{6,5},{7,6},{0,7},{9,8},{10,9},{11,1... | collective-permute-start | bytes 416 | tf_op jit(solution)/shard_map/ppermute | solution.py:15
  137.8 0.9 collective-permute-done.6
  139.4 10.2 %fusion.53 = f32[17,32768]{1,0:T(8,128)S(1)} fusion(f32[17,2]{1,0:T(8,128)} %copy-done.11, f32[17,32768]{1,0:T(8,128)} %copy-done, f32[17,2]{1,0:T(8,128)S(1)} %collective-permute-done.6, f32[32768]{0:T(1024)} %bitcast.111, f32[32768]{0:T(1024)} %bitcast.112, f32[32768]{0:T(1024)} %bitcast.108, f32[17]{0:T(128)} %get-tuple-element.80, f32[32768]{0:T(1024)} %bitcast.109, ...), kind=kLoop, calls=%fused_computation.94 | loop fusion | flops 15597568 | bytes 5177684 | tf_op jit(solution)/shard_map/mul | solution.py:35
  151.1 3.9 %collective-permute-start.9 = (f32[17,2]{1,0:T(8,128)S(1)}, f32[17,2]{1,0:T(8,128)}, u32[]{:S(2)}, u32[]{:S(2)}) collective-permute-start(f32[17,2]{1,0:T(8,128)S(1)} %get-tuple-element.51), channel_id=1, source_target_pairs={{1,0},{2,1},{3,2},{4,3},{5,4},{6,5},{7,6},{0,7},{9,8},{10,9},{11,1... | collective-permute-start | bytes 416 | tf_op jit(solution)/shard_map/ppermute | solution.py:15
  155.7 1.4 eq.264
  157.1 6.4 %fusion.45 = f32[17,32768]{1,0:T(8,128)S(1)} fusion(f32[17,2]{1,0:T(8,128)} %collective-permute-done.9, f32[17,32768]{1,0:T(8,128)S(1)} %fusion.53, f32[17,2]{1,0:T(8,128)} %collective-permute-done.8, f32[32768]{0:T(1024)} %bitcast.106, f32[32768]{0:T(1024)} %bitcast.107, f32[32768]{0:T(1024)} %bitcast.103, f32[17]{0:T(128)} %get-tuple-element.81, ...), kind=kLoop, calls=%fused_computation.84 | loop fusion | flops 15597568 | bytes 5177684 | tf_op jit(solution)/shard_map/mul | solution.py:35
  163.6 1.6 copy-done.1
  166.0 3.9 %collective-permute-start.11 = (f32[17,2]{1,0:T(8,128)S(1)}, f32[17,2]{1,0:T(8,128)S(1)}, u32[]{:S(2)}, u32[]{:S(2)}) collective-permute-start(f32[17,2]{1,0:T(8,128)S(1)} %get-tuple-element.49), channel_id=1, source_target_pairs={{1,0},{2,1},{3,2},{4,3},{5,4},{6,5},{7,6},{0,7},{9,8},{10,9},{11,1... | collective-permute-start | bytes 416 | tf_op jit(solution)/shard_map/ppermute | solution.py:15
  171.7 10.1 %fusion.37 = f32[17,32768]{1,0:T(8,128)S(1)} fusion(f32[17,2]{1,0:T(8,128)S(1)} %collective-permute-done.11, f32[17,32768]{1,0:T(8,128)} %copy-done.1, f32[17,2]{1,0:T(8,128)S(1)} %collective-permute-done.10, f32[32768]{0:T(1024)} %bitcast.101, f32[32768]{0:T(1024)} %bitcast.102, f32[32768]{0:T(1024)} %bitcast.98, f32[17]{0:T(128)S(1)} %copy-done.17, ...), kind=kLoop, calls=%fused_computation.74 | loop fusion | flops 15597568 | bytes 5177684 | tf_op jit(solution)/shard_map/mul | solution.py:35
  182.7 4.0 %collective-permute-start.13 = (f32[17,2]{1,0:T(8,128)S(1)}, f32[17,2]{1,0:T(8,128)S(1)}, u32[]{:S(2)}, u32[]{:S(2)}) collective-permute-start(f32[17,2]{1,0:T(8,128)S(1)} %get-tuple-element.47), channel_id=1, source_target_pairs={{1,0},{2,1},{3,2},{4,3},{5,4},{6,5},{7,6},{0,7},{9,8},{10,9},{11,1... | collective-permute-start | bytes 416 | tf_op jit(solution)/shard_map/ppermute | solution.py:15
  186.7 2.4 %fusion.82 = (f32[1,1,32768]{2,1,0:T(1,128)}, f32[1,1,32768]{2,1,0:T(1,128)S(1)}) fusion(f32[8,5,32768]{2,1,0:T(8,128)} %all-gather.2.cloned.1.call-done), kind=kLoop, calls=%fused_computation.158 | loop fusion | bytes 524288 | tf_op jit(solution)/shard_map/slice | solution.py:26
  189.2 5.4 %fusion.29 = f32[17,32768]{1,0:T(8,128)S(1)} fusion(f32[17,2]{1,0:T(8,128)S(1)} %collective-permute-done.13, f32[17,32768]{1,0:T(8,128)S(1)} %fusion.37, f32[17,2]{1,0:T(8,128)S(1)} %collective-permute-done.12, f32[32768]{0:T(1024)S(1)} %bitcast.96, f32[32768]{0:T(1024)S(1)} %bitcast.97, f32[32768]{0:T(1024)S(1)} %bitcast.94, f32[17]{0:T(128)S(1)} %copy-done.15, ...), kind=kLoop, calls=%fused_computation.64 | loop fusion | flops 15597568 | bytes 5177684 | tf_op jit(solution)/shard_map/mul | solution.py:35
  195.6 4.4 %collective-permute-start.15 = (f32[17,2]{1,0:T(8,128)S(1)}, f32[17,2]{1,0:T(8,128)}, u32[]{:S(2)}, u32[]{:S(2)}) collective-permute-start(f32[17,2]{1,0:T(8,128)S(1)} %get-tuple-element.45), channel_id=1, source_target_pairs={{1,0},{2,1},{3,2},{4,3},{5,4},{6,5},{7,6},{0,7},{9,8},{10,9},{11,1... | collective-permute-start | bytes 416 | tf_op jit(solution)/shard_map/ppermute | solution.py:15
  200.7 1.4 eq.303
  202.1 6.4 %fusion.21 = f32[17,32768]{1,0:T(8,128)S(1)} fusion(f32[17,2]{1,0:T(8,128)} %collective-permute-done.15, f32[17,32768]{1,0:T(8,128)S(1)} %fusion.29, f32[17,2]{1,0:T(8,128)} %collective-permute-done.14, f32[32768]{0:T(1024)S(1)} %bitcast.92, f32[32768]{0:T(1024)} %bitcast.93, f32[32768]{0:T(1024)} %bitcast.129, f32[17]{0:T(128)} %get-tuple-element.76, ...), kind=kLoop, calls=%fused_computation.54 | loop fusion | flops 15597568 | bytes 5177684 | tf_op jit(solution)/shard_map/mul | solution.py:35
  208.6 1.8 multiply_reduce_fusion
  210.4 21.6 %psum.7 = f32[16]{0:T(128)S(1)} all-reduce(f32[16]{0:T(128)S(1)} %get-tuple-element.2), channel_id=1, replica_groups=mesh['bump'=4,'nx'=2,'ny'=4] {'nx','ny'}, use_global_device_ids=true, to_apply=%region_1.2 | all-reduce | flops 16 | bytes 128 | tf_op jit(solution)/shard_map/psum | solution.py:61
  (115 shorter events, 20.9 us)
Async XLA Ops:
  7.2 16.4 %copy-start.22 = (f32[16]{0:T(128)S(1)}, f32[16]{0:T(128)}, u32[]{:S(2)}) copy-start(f32[16]{0:T(128)} %param.13) | copy-start | bytes 196
  7.2 16.4 %copy-start.21 = (s32[16]{0:T(128)S(1)}, s32[16]{0:T(128)}, u32[]{:S(2)}) copy-start(s32[16]{0:T(128)} %param.12) | copy-start | bytes 196
  7.2 64.7 %all-gather.2.cloned.1.call-start = ((), (), s32[]{:S(2)}) async-start(), calls=%async_computation | async-start | bytes 10485760 | tf_op jit(solution)/shard_map/all_gather | solution.py:50
  10.8 81.5 %collective-permute-start.1 = (f32[17,2]{1,0:T(8,128)S(1)}, f32[17,2]{1,0:T(8,128)S(1)}, u32[]{:S(2)}, u32[]{:S(2)}) collective-permute-start(f32[17,2]{1,0:T(8,128)S(1)} %broadcast_in_dim.178), channel_id=1, source_target_pairs={{1,0},{2,1},{3,2},{4,3},{5,4},{6,5},{7,6},{0,7},{9,8},{10,9},{11,1... | collective-permute-start | bytes 416 | tf_op jit(solution)/shard_map/ppermute | solution.py:15
  16.9 75.5 %collective-permute-start = (f32[17,2]{1,0:T(8,128)S(1)}, f32[17,2]{1,0:T(8,128)S(1)}, u32[]{:S(2)}, u32[]{:S(2)}) collective-permute-start(f32[17,2]{1,0:T(8,128)S(1)} %broadcast_in_dim.175), channel_id=1, source_target_pairs={{0,1},{1,2},{2,3},{3,4},{4,5},{5,6},{6,7},{7,0},{8,9},{9,10},{10,1... | collective-permute-start | bytes 416 | tf_op jit(solution)/shard_map/ppermute | solution.py:14
  99.7 6.4 %collective-permute-start.2 = (f32[17,2]{1,0:T(8,128)S(1)}, f32[17,2]{1,0:T(8,128)S(1)}, u32[]{:S(2)}, u32[]{:S(2)}) collective-permute-start(f32[17,2]{1,0:T(8,128)S(1)} %get-tuple-element.56), channel_id=1, source_target_pairs={{0,1},{1,2},{2,3},{3,4},{4,5},{5,6},{6,7},{7,0},{8,9},{9,10},{10,1... | collective-permute-start | bytes 416 | tf_op jit(solution)/shard_map/ppermute | solution.py:14
  101.1 4.9 %collective-permute-start.3 = (f32[17,2]{1,0:T(8,128)S(1)}, f32[17,2]{1,0:T(8,128)S(1)}, u32[]{:S(2)}, u32[]{:S(2)}) collective-permute-start(f32[17,2]{1,0:T(8,128)S(1)} %get-tuple-element.57), channel_id=1, source_target_pairs={{1,0},{2,1},{3,2},{4,3},{5,4},{6,5},{7,6},{0,7},{9,8},{10,9},{11,1... | collective-permute-start | bytes 416 | tf_op jit(solution)/shard_map/ppermute | solution.py:15
  106.6 15.5 %copy-start.19 = (pred[128]{0:T(512)(128)(4,1)S(1)}, pred[128]{0:T(512)(128)(4,1)}, u32[]{:S(2)}) copy-start(pred[128]{0:T(512)(128)(4,1)} %get-tuple-element.70) | copy-start | bytes 388
  117.4 6.8 %collective-permute-start.4 = (f32[17,2]{1,0:T(8,128)}, f32[17,2]{1,0:T(8,128)}, u32[]{:S(2)}, u32[]{:S(2)}) collective-permute-start(f32[17,2]{1,0:T(8,128)} %get-tuple-element.54), channel_id=1, source_target_pairs={{0,1},{1,2},{2,3},{3,4},{4,5},{5,6},{6,7},{7,0},{8,9},{9,10},{10,1... | collective-permute-start | bytes 416 | tf_op jit(solution)/shard_map/ppermute | solution.py:14
  117.7 6.5 %collective-permute-start.5 = (f32[17,2]{1,0:T(8,128)S(1)}, f32[17,2]{1,0:T(8,128)}, u32[]{:S(2)}, u32[]{:S(2)}) collective-permute-start(f32[17,2]{1,0:T(8,128)S(1)} %get-tuple-element.55), channel_id=1, source_target_pairs={{1,0},{2,1},{3,2},{4,3},{5,4},{6,5},{7,6},{0,7},{9,8},{10,9},{11,1... | collective-permute-start | bytes 416 | tf_op jit(solution)/shard_map/ppermute | solution.py:15
  124.3 12.9 %copy-start.18 = (pred[128]{0:T(512)(128)(4,1)S(1)}, pred[128]{0:T(512)(128)(4,1)}, u32[]{:S(2)}) copy-start(pred[128]{0:T(512)(128)(4,1)} %get-tuple-element.71) | copy-start | bytes 388
  132.4 6.4 %collective-permute-start.6 = (f32[17,2]{1,0:T(8,128)S(1)}, f32[17,2]{1,0:T(8,128)S(1)}, u32[]{:S(2)}, u32[]{:S(2)}) collective-permute-start(f32[17,2]{1,0:T(8,128)S(1)} %get-tuple-element.52), channel_id=1, source_target_pairs={{0,1},{1,2},{2,3},{3,4},{4,5},{5,6},{6,7},{7,0},{8,9},{9,10},{10,1... | collective-permute-start | bytes 416 | tf_op jit(solution)/shard_map/ppermute | solution.py:14
  133.2 5.6 %collective-permute-start.7 = (f32[17,2]{1,0:T(8,128)S(1)}, f32[17,2]{1,0:T(8,128)S(1)}, u32[]{:S(2)}, u32[]{:S(2)}) collective-permute-start(f32[17,2]{1,0:T(8,128)S(1)} %get-tuple-element.53), channel_id=1, source_target_pairs={{1,0},{2,1},{3,2},{4,3},{5,4},{6,5},{7,6},{0,7},{9,8},{10,9},{11,1... | collective-permute-start | bytes 416 | tf_op jit(solution)/shard_map/ppermute | solution.py:15
  139.4 15.6 %copy-start.16 = (pred[128]{0:T(512)(128)(4,1)S(1)}, pred[128]{0:T(512)(128)(4,1)}, u32[]{:S(2)}) copy-start(pred[128]{0:T(512)(128)(4,1)} %get-tuple-element.72) | copy-start | bytes 388
  150.3 6.8 %collective-permute-start.8 = (f32[17,2]{1,0:T(8,128)}, f32[17,2]{1,0:T(8,128)}, u32[]{:S(2)}, u32[]{:S(2)}) collective-permute-start(f32[17,2]{1,0:T(8,128)} %get-tuple-element.50), channel_id=1, source_target_pairs={{0,1},{1,2},{2,3},{3,4},{4,5},{5,6},{6,7},{7,0},{8,9},{9,10},{10,1... | collective-permute-start | bytes 416 | tf_op jit(solution)/shard_map/ppermute | solution.py:14
  151.1 6.0 %collective-permute-start.9 = (f32[17,2]{1,0:T(8,128)S(1)}, f32[17,2]{1,0:T(8,128)}, u32[]{:S(2)}, u32[]{:S(2)}) collective-permute-start(f32[17,2]{1,0:T(8,128)S(1)} %get-tuple-element.51), channel_id=1, source_target_pairs={{1,0},{2,1},{3,2},{4,3},{5,4},{6,5},{7,6},{0,7},{9,8},{10,9},{11,1... | collective-permute-start | bytes 416 | tf_op jit(solution)/shard_map/ppermute | solution.py:15
  157.1 12.9 %copy-start.14 = (pred[128]{0:T(512)(128)(4,1)S(1)}, pred[128]{0:T(512)(128)(4,1)}, u32[]{:S(2)}) copy-start(pred[128]{0:T(512)(128)(4,1)} %get-tuple-element.73) | copy-start | bytes 388
  157.1 14.6 %copy-start.17 = (f32[17]{0:T(128)S(1)}, f32[17]{0:T(128)}, u32[]{:S(2)}) copy-start(f32[17]{0:T(128)} %get-tuple-element.82) | copy-start | bytes 208
  165.2 6.4 %collective-permute-start.10 = (f32[17,2]{1,0:T(8,128)S(1)}, f32[17,2]{1,0:T(8,128)S(1)}, u32[]{:S(2)}, u32[]{:S(2)}) collective-permute-start(f32[17,2]{1,0:T(8,128)S(1)} %get-tuple-element.48), channel_id=1, source_target_pairs={{0,1},{1,2},{2,3},{3,4},{4,5},{5,6},{6,7},{7,0},{8,9},{9,10},{10,1... | collective-permute-start | bytes 416 | tf_op jit(solution)/shard_map/ppermute | solution.py:14
  166.0 5.6 %collective-permute-start.11 = (f32[17,2]{1,0:T(8,128)S(1)}, f32[17,2]{1,0:T(8,128)S(1)}, u32[]{:S(2)}, u32[]{:S(2)}) collective-permute-start(f32[17,2]{1,0:T(8,128)S(1)} %get-tuple-element.49), channel_id=1, source_target_pairs={{1,0},{2,1},{3,2},{4,3},{5,4},{6,5},{7,6},{0,7},{9,8},{10,9},{11,1... | collective-permute-start | bytes 416 | tf_op jit(solution)/shard_map/ppermute | solution.py:15
  171.6 17.5 %copy-start.3 = (f32[1,1,32768]{2,1,0:T(1,128)S(1)}, f32[1,1,32768]{2,1,0:T(1,128)}, u32[]{:S(2)}) copy-start(f32[1,1,32768]{2,1,0:T(1,128)} %get-tuple-element.40) | copy-start | bytes 393220
  171.6 17.5 %copy-start.4 = (f32[1,1,32768]{2,1,0:T(1,128)S(1)}, f32[1,1,32768]{2,1,0:T(1,128)}, u32[]{:S(2)}) copy-start(f32[1,1,32768]{2,1,0:T(1,128)} %get-tuple-element.41) | copy-start | bytes 393220
  171.7 17.5 %copy-start.5 = (f32[1,1,32768]{2,1,0:T(1,128)S(1)}, f32[1,1,32768]{2,1,0:T(1,128)}, u32[]{:S(2)}) copy-start(f32[1,1,32768]{2,1,0:T(1,128)} %get-tuple-element.7) | copy-start | bytes 393220
  171.7 17.5 %copy-start.6 = (f32[1,1,32768]{2,1,0:T(1,128)S(1)}, f32[1,1,32768]{2,1,0:T(1,128)}, u32[]{:S(2)}) copy-start(f32[1,1,32768]{2,1,0:T(1,128)} %get-tuple-element.8) | copy-start | bytes 393220
  171.7 17.5 %copy-start.8 = (pred[32768]{0:T(1024)(128)(4,1)S(1)}, pred[32768]{0:T(1024)(128)(4,1)}, u32[]{:S(2)}) copy-start(pred[32768]{0:T(1024)(128)(4,1)} %eq.300) | copy-start | bytes 98308
  171.7 17.5 %copy-start.9 = (pred[32768]{0:T(1024)(128)(4,1)S(1)}, pred[32768]{0:T(1024)(128)(4,1)}, u32[]{:S(2)}) copy-start(pred[32768]{0:T(1024)(128)(4,1)} %eq.261) | copy-start | bytes 98308
  171.7 17.5 %copy-start.15 = (f32[17]{0:T(128)S(1)}, f32[17]{0:T(128)}, u32[]{:S(2)}) copy-start(f32[17]{0:T(128)} %get-tuple-element.83) | copy-start | bytes 208
  181.9 7.2 %collective-permute-start.12 = (f32[17,2]{1,0:T(8,128)S(1)}, f32[17,2]{1,0:T(8,128)S(1)}, u32[]{:S(2)}, u32[]{:S(2)}) collective-permute-start(f32[17,2]{1,0:T(8,128)S(1)} %get-tuple-element.46), channel_id=1, source_target_pairs={{0,1},{1,2},{2,3},{3,4},{4,5},{5,6},{6,7},{7,0},{8,9},{9,10},{10,1... | collective-permute-start | bytes 416 | tf_op jit(solution)/shard_map/ppermute | solution.py:14
  182.7 6.4 %collective-permute-start.13 = (f32[17,2]{1,0:T(8,128)S(1)}, f32[17,2]{1,0:T(8,128)S(1)}, u32[]{:S(2)}, u32[]{:S(2)}) collective-permute-start(f32[17,2]{1,0:T(8,128)S(1)} %get-tuple-element.47), channel_id=1, source_target_pairs={{1,0},{2,1},{3,2},{4,3},{5,4},{6,5},{7,6},{0,7},{9,8},{10,9},{11,1... | collective-permute-start | bytes 416 | tf_op jit(solution)/shard_map/ppermute | solution.py:15
  195.3 6.8 %collective-permute-start.14 = (f32[17,2]{1,0:T(8,128)}, f32[17,2]{1,0:T(8,128)}, u32[]{:S(2)}, u32[]{:S(2)}) collective-permute-start(f32[17,2]{1,0:T(8,128)} %get-tuple-element.44), channel_id=1, source_target_pairs={{0,1},{1,2},{2,3},{3,4},{4,5},{5,6},{6,7},{7,0},{8,9},{9,10},{10,1... | collective-permute-start | bytes 416 | tf_op jit(solution)/shard_map/ppermute | solution.py:14
  195.6 6.5 %collective-permute-start.15 = (f32[17,2]{1,0:T(8,128)S(1)}, f32[17,2]{1,0:T(8,128)}, u32[]{:S(2)}, u32[]{:S(2)}) collective-permute-start(f32[17,2]{1,0:T(8,128)S(1)} %get-tuple-element.45), channel_id=1, source_target_pairs={{1,0},{2,1},{3,2},{4,3},{5,4},{6,5},{7,6},{0,7},{9,8},{10,9},{11,1... | collective-permute-start | bytes 416 | tf_op jit(solution)/shard_map/ppermute | solution.py:15
  208.5 23.5 %copy-start.23 = (f32[16]{0:T(128)S(1)}, f32[16]{0:T(128)}, u32[]{:S(2)}) copy-start(f32[16]{0:T(128)} %param.13) | copy-start | bytes 196
  (9 other events, 35.6 us)
Sparse Core Ops, SparseCore 0:
  10.9 60.9 all-gather.1
where the time goes:
time: 240 us; the launch traced here: 239 us
  other arithmetic  63.7 us (27%)
  waiting for transfers between devices  50.4 us (21%)
  local copies, waits for them, and re-layouts  50.1 us (21%)
  starting transfers between devices  39.2 us (16%)
  blocking collectives  21.6 us (9%)
  between operations  14.5 us (6%)
    mul x8, other arithmetic, advance(): return table[0] * mixed  60.6 us
    all_gather x1, waiting for transfers between devices, on_device(): all_tables = lax.all_gather(tables, 'bump', axis=0, tiled=True)  47.5 us
    ppermute x8, starting transfers between devices, with_halo(): after = lax.ppermute(initial, axis, down)  33.9 us
    psum x1, blocking collectives, on_device(): totals = lax.psum(partial_sums, ('nx', 'ny'))  21.6 us
    slice x2, local copies, waits for them, and re-layouts, advance(): upward = table[1] + variance * table[2]  12.5 us
    slice x1, local copies, waits for them, and re-layouts, advance(): return table[0] * mixed  10.3 us
    unnamed x49, local copies, waits for them, and re-layouts  9.57 us
    eq x8, local copies, waits for them, and re-layouts, advance(): branch_nodes == -1  5.98 us
  transfers between devices with their start and end apart: 17, of which 4 were waited for; matrix products, arithmetic and copies ran while one was open for 16% of the time, Pallas kernels for 0%

commit v1 on v0

--- a/solution.py
+++ b/solution.py
@@ -58,7 +58,7 @@
     base_values = values[0]
     bumped_values = values[1:]
     partial_sums = jnp.sum(positions[None, :] * (bumped_values - base_values[None, :]), axis=1)
-    totals = lax.psum(partial_sums, ("nx", "ny"))
+    totals = jnp.sum(lax.all_gather(partial_sums, ("nx", "ny")), axis=0)
     return (bumped_values, totals / bump_size)
 
 

time: 240 us -> 231 us (0.963)
  other arithmetic: 63.7 us -> 57.7 us
  local copies, waits for them, and re-layouts: 50.1 us -> 45.4 us
    unnamed x0 -> x1, blocking collectives: none -> 21.9 us
    psum x1 -> x0, blocking collectives: 21.6 us -> none  [on_device(): totals = lax.psum(partial_sums, ('nx', 'ny'))]
    mul x8, other arithmetic: 60.6 us -> 54.7 us  [advance(): return table[0] * mixed]
    ppermute x8, waiting for transfers between devices: 2.83 us -> 6.7 us  [with_halo(): before = lax.ppermute(last, axis, up)]
    all_gather x1, waiting for transfers between devices: 47.5 us -> 44.7 us  [on_device(): all_tables = lax.all_gather(tables, 'bump', axis=0, tiled=True)]
    unnamed x49 -> x66, local copies, waits for them, and re-layouts: 9.57 us -> 8.83 us
  transfers between devices with their start and end apart: 17 -> 17, of which waited for: 4 -> 6; matrix products, arithmetic and copies ran while one was open for 16% -> 15% of each run, Pallas kernels for 0% -> 0%
where the time goes in v1:
time: 231 us
  other arithmetic  57.7 us (25%)
  waiting for transfers between devices  51.5 us (22%)
  local copies, waits for them, and re-layouts  45.4 us (20%)
  starting transfers between devices  39.2 us (17%)
  blocking collectives  21.9 us (9%)
  between operations  15.3 us (7%)
    mul x8, other arithmetic, advance(): return table[0] * mixed  54.7 us
    all_gather x1, waiting for transfers between devices, on_device(): all_tables = lax.all_gather(tables, 'bump', axis=0, tiled=True)  44.7 us
    ppermute x8, starting transfers between devices, with_halo(): after = lax.ppermute(initial, axis, down)  33 us
    unnamed x1, blocking collectives  21.9 us
    slice x2, local copies, waits for them, and re-layouts, advance(): upward = table[1] + variance * table[2]  11.8 us
    slice x1, local copies, waits for them, and re-layouts, advance(): return table[0] * mixed  10.3 us
    unnamed x66, local copies, waits for them, and re-layouts  8.83 us
    ppermute x8, waiting for transfers between devices, with_halo(): before = lax.ppermute(last, axis, up)  6.7 us
  transfers between devices with their start and end apart: 17, of which 6 were waited for; matrix products, arithmetic and copies ran while one was open for 15% of the time, Pallas kernels for 0%

profile of v1, /device:TPU:0, one launch (start us, length us, event | category | flops | bytes accessed | tf_op | source)
XLA Modules:
  0.0 231.0 jit_solution(3953195959726328601)
XLA Ops:
  7.3 3.5 %copy.10 = f32[2,5,32768]{2,1,0:T(8,128)} copy(f32[2,5,32768]{2,0,1:T(2,128)} %param.9) | data formatting | bytes 2621440 | tf_op args[2]
  10.8 6.0 %collective-permute-start.1 = (f32[17,2]{1,0:T(8,128)S(1)}, f32[17,2]{1,0:T(8,128)S(1)}, u32[]{:S(2)}, u32[]{:S(2)}) collective-permute-start(f32[17,2]{1,0:T(8,128)S(1)} %broadcast_in_dim.178), channel_id=1, source_target_pairs={{1,0},{2,1},{3,2},{4,3},{5,4},{6,5},{7,6},{0,7},{9,8},{10,9},{11,1... | collective-permute-start | bytes 416 | tf_op jit(solution)/shard_map/ppermute | solution.py:15
  27.2 44.7 %all-gather.3.cloned.1.call-done = f32[8,5,32768]{2,1,0:T(8,128)} async-done(((f32[2,5,32768]{2,1,0:T(8,128)}), f32[8,5,32768]{2,1,0:T(8,128)}) %all-gather.3.cloned.1.call-update) | async-done | bytes 5242896 | tf_op jit(solution)/shard_map/all_gather | solution.py:50
  71.9 10.0 %fusion.81 = (f32[1,1,32768]{2,1,0:T(1,128)S(1)}, f32[1,1,32768]{2,1,0:T(1,128)S(1)}, f32[1,1,32768]{2,1,0:T(1,128)}, f32[1,1,32768]{2,1,0:T(1,128)}, f32[1,1,32...) fusion(f32[8,5,32768]{2,1,0:T(8,128)} %all-gather.3.cloned.1.ca, ...), kind=kLoop, calls=%fused_computation.157 | loop fusion | bytes 4980736 | tf_op jit(solution)/shard_map/slice | solution.py:26
  81.9 10.3 %fusion.80 = (f32[1,1,32768]{2,1,0:T(1,128)S(1)}, f32[1,1,32768]{2,1,0:T(1,128)S(1)}, f32[1,1,32768]{2,1,0:T(1,128)}, f32[1,1,32768]{2,1,0:T(1,128)}, f32[1,1,32...) fusion(f32[8,5,32768]{2,1,0:T(8,128)} %all-gather.3.cloned.1.ca, ...), kind=kLoop, calls=%fused_computation.156 | loop fusion | bytes 4980736 | tf_op jit(solution)/shard_map/slice | solution.py:35
  92.5 5.4 %fusion.77 = f32[17,32768]{1,0:T(8,128)S(1)} fusion(f32[17,2]{1,0:T(8,128)S(1)} %collective-permute-done.1, f32[17,32768]{1,0:T(8,128)S(1)} %broadcast_in_dim.174, f32[17,2]{1,0:T(8,128)S(1)} %collective-permute-done, f32[32768]{0:T(1024)S(1)} %bitcast.125, f32[32768]{0:T(1024)S(1)} %bitcast.126, f32[32768]{0:T(1024)S(1)} %bitcast.127, ...), kind=kLoop, calls=%fused_computation.124 | loop fusion | flops 15597568 | bytes 5177684 | tf_op jit(solution)/shard_map/mul | solution.py:35
  97.9 1.6 copy-done
  99.6 1.5 collective-permute-start.2
  101.1 3.2 %collective-permute-start.3 = (f32[17,2]{1,0:T(8,128)S(1)}, f32[17,2]{1,0:T(8,128)S(1)}, u32[]{:S(2)}, u32[]{:S(2)}) collective-permute-start(f32[17,2]{1,0:T(8,128)S(1)} %get-tuple-element.57), channel_id=1, source_target_pairs={{1,0},{2,1},{3,2},{4,3},{5,4},{6,5},{7,6},{0,7},{9,8},{10,9},{11,1... | collective-permute-start | bytes 416 | tf_op jit(solution)/shard_map/ppermute | solution.py:15
  105.1 0.9 collective-permute-done.2
  106.6 10.0 %fusion.69 = f32[17,32768]{1,0:T(8,128)S(1)} fusion(f32[17,2]{1,0:T(8,128)} %copy-done.20, f32[17,32768]{1,0:T(8,128)} %copy-done, f32[17,2]{1,0:T(8,128)S(1)} %collective-permute-done.2, f32[32768]{0:T(1024)} %bitcast.122, f32[32768]{0:T(1024)} %bitcast.123, f32[32768]{0:T(1024)} %bitcast.119, f32[17]{0:T(128)} %get-tuple-element.78, f32[32768]{0:T(1024)} %bitcast.120, ...), kind=kLoop, calls=%fused_computation.114 | loop fusion | flops 15597568 | bytes 5177684 | tf_op jit(solution)/shard_map/mul | solution.py:35
  117.6 4.5 %collective-permute-start.5 = (f32[17,2]{1,0:T(8,128)S(1)}, f32[17,2]{1,0:T(8,128)}, u32[]{:S(2)}, u32[]{:S(2)}) collective-permute-start(f32[17,2]{1,0:T(8,128)S(1)} %get-tuple-element.55), channel_id=1, source_target_pairs={{1,0},{2,1},{3,2},{4,3},{5,4},{6,5},{7,6},{0,7},{9,8},{10,9},{11,1... | collective-permute-start | bytes 416 | tf_op jit(solution)/shard_map/ppermute | solution.py:15
  122.7 1.4 eq.261
  124.1 6.4 %fusion.61 = f32[17,32768]{1,0:T(8,128)S(1)} fusion(f32[17,2]{1,0:T(8,128)} %collective-permute-done.5, f32[17,32768]{1,0:T(8,128)S(1)} %fusion.69, f32[17,2]{1,0:T(8,128)} %collective-permute-done.4, f32[32768]{0:T(1024)} %bitcast.117, f32[32768]{0:T(1024)} %bitcast.118, f32[32768]{0:T(1024)} %bitcast.114, f32[17]{0:T(128)} %get-tuple-element.79, ...), kind=kLoop, calls=%fused_computation.104 | loop fusion | flops 15597568 | bytes 5177684 | tf_op jit(solution)/shard_map/mul | solution.py:35
  130.6 1.6 copy-done.1
  133.1 3.9 %collective-permute-start.7 = (f32[17,2]{1,0:T(8,128)S(1)}, f32[17,2]{1,0:T(8,128)S(1)}, u32[]{:S(2)}, u32[]{:S(2)}) collective-permute-start(f32[17,2]{1,0:T(8,128)S(1)} %get-tuple-element.53), channel_id=1, source_target_pairs={{1,0},{2,1},{3,2},{4,3},{5,4},{6,5},{7,6},{0,7},{9,8},{10,9},{11,1... | collective-permute-start | bytes 416 | tf_op jit(solution)/shard_map/ppermute | solution.py:15
  137.0 1.7 collective-permute-done.6
  139.3 10.0 %fusion.53 = f32[17,32768]{1,0:T(8,128)S(1)} fusion(f32[17,2]{1,0:T(8,128)} %copy-done.21, f32[17,32768]{1,0:T(8,128)} %copy-done.1, f32[17,2]{1,0:T(8,128)S(1)} %collective-permute-done.6, f32[32768]{0:T(1024)} %bitcast.112, f32[32768]{0:T(1024)} %bitcast.113, f32[32768]{0:T(1024)} %bitcast.109, f32[17]{0:T(128)} %get-tuple-element.80, f32[32768]{0:T(1024)} %bitcast.110, ...), kind=kLoop, calls=%fused_computation.94 | loop fusion | flops 15597568 | bytes 5177684 | tf_op jit(solution)/shard_map/mul | solution.py:35
  150.8 3.9 %collective-permute-start.9 = (f32[17,2]{1,0:T(8,128)S(1)}, f32[17,2]{1,0:T(8,128)}, u32[]{:S(2)}, u32[]{:S(2)}) collective-permute-start(f32[17,2]{1,0:T(8,128)S(1)} %get-tuple-element.51), channel_id=1, source_target_pairs={{1,0},{2,1},{3,2},{4,3},{5,4},{6,5},{7,6},{0,7},{9,8},{10,9},{11,1... | collective-permute-start | bytes 416 | tf_op jit(solution)/shard_map/ppermute | solution.py:15
  154.7 2.0 collective-permute-done.8
  156.8 6.6 %fusion.45 = f32[17,32768]{1,0:T(8,128)S(1)} fusion(f32[17,2]{1,0:T(8,128)} %collective-permute-done.9, f32[17,32768]{1,0:T(8,128)S(1)} %fusion.53, f32[17,2]{1,0:T(8,128)} %collective-permute-done.8, f32[32768]{0:T(1024)} %bitcast.107, f32[32768]{0:T(1024)} %bitcast.108, f32[32768]{0:T(1024)} %bitcast.104, f32[17]{0:T(128)} %get-tuple-element.81, ...), kind=kLoop, calls=%fused_computation.84 | loop fusion | flops 15597568 | bytes 5177684 | tf_op jit(solution)/shard_map/mul | solution.py:35
  164.3 3.8 %collective-permute-start.11 = (f32[17,2]{1,0:T(8,128)S(1)}, f32[17,2]{1,0:T(8,128)S(1)}, u32[]{:S(2)}, u32[]{:S(2)}) collective-permute-start(f32[17,2]{1,0:T(8,128)S(1)} %get-tuple-element.49), channel_id=1, source_target_pairs={{1,0},{2,1},{3,2},{4,3},{5,4},{6,5},{7,6},{0,7},{9,8},{10,9},{11,1... | collective-permute-start | bytes 416 | tf_op jit(solution)/shard_map/ppermute | solution.py:15
  168.7 1.1 collective-permute-done.10
  169.9 5.4 %fusion.37 = f32[17,32768]{1,0:T(8,128)S(1)} fusion(f32[17,2]{1,0:T(8,128)S(1)} %collective-permute-done.11, f32[17,32768]{1,0:T(8,128)S(1)} %fusion.45, f32[17,2]{1,0:T(8,128)S(1)} %collective-permute-done.10, f32[32768]{0:T(1024)S(1)} %bitcast.102, f32[32768]{0:T(1024)S(1)} %bitcast.103, f32[32768]{0:T(1024)S(1)} %bitcast.99, f32[17]{0:T(128)S(1)} %copy-done.24, ...), kind=kLoop, calls=%fused_computation.74 | loop fusion | flops 15597568 | bytes 5177684 | tf_op jit(solution)/shard_map/mul | solution.py:35
  176.3 3.9 %collective-permute-start.13 = (f32[17,2]{1,0:T(8,128)S(1)}, f32[17,2]{1,0:T(8,128)S(1)}, u32[]{:S(2)}, u32[]{:S(2)}) collective-permute-start(f32[17,2]{1,0:T(8,128)S(1)} %get-tuple-element.47), channel_id=1, source_target_pairs={{1,0},{2,1},{3,2},{4,3},{5,4},{6,5},{7,6},{0,7},{9,8},{10,9},{11,1... | collective-permute-start | bytes 416 | tf_op jit(solution)/shard_map/ppermute | solution.py:15
  180.2 1.8 fusion.82
  182.1 5.4 %fusion.29 = f32[17,32768]{1,0:T(8,128)S(1)} fusion(f32[17,2]{1,0:T(8,128)S(1)} %collective-permute-done.13, f32[17,32768]{1,0:T(8,128)S(1)} %fusion.37, f32[17,2]{1,0:T(8,128)S(1)} %collective-permute-done.12, f32[32768]{0:T(1024)S(1)} %bitcast.97, f32[32768]{0:T(1024)S(1)} %bitcast.98, f32[32768]{0:T(1024)S(1)} %bitcast.95, f32[17]{0:T(128)S(1)} %copy-done.23, ...), kind=kLoop, calls=%fused_computation.64 | loop fusion | flops 15597568 | bytes 5177684 | tf_op jit(solution)/shard_map/mul | solution.py:35
  188.5 3.8 %collective-permute-start.15 = (f32[17,2]{1,0:T(8,128)S(1)}, f32[17,2]{1,0:T(8,128)S(1)}, u32[]{:S(2)}, u32[]{:S(2)}) collective-permute-start(f32[17,2]{1,0:T(8,128)S(1)} %get-tuple-element.45), channel_id=1, source_target_pairs={{1,0},{2,1},{3,2},{4,3},{5,4},{6,5},{7,6},{0,7},{9,8},{10,9},{11,1... | collective-permute-start | bytes 416 | tf_op jit(solution)/shard_map/ppermute | solution.py:15
  193.0 1.0 collective-permute-done.14
  194.0 5.4 %fusion.21 = f32[17,32768]{1,0:T(8,128)S(1)} fusion(f32[17,2]{1,0:T(8,128)S(1)} %collective-permute-done.15, f32[17,32768]{1,0:T(8,128)S(1)} %fusion.29, f32[17,2]{1,0:T(8,128)S(1)} %collective-permute-done.14, f32[32768]{0:T(1024)S(1)} %bitcast.93, f32[32768]{0:T(1024)S(1)} %bitcast.94, f32[32768]{0:T(1024)S(1)} %bitcast.130, f32[17]{0:T(128)S(1)} %get-tuple-element.76, ...), kind=kLoop, calls=%fused_computation.54 | loop fusion | flops 15597568 | bytes 5177684 | tf_op jit(solution)/shard_map/mul | solution.py:35
  199.6 1.8 multiply_reduce_fusion
  201.6 21.9 %all-reduce = f32[128]{0:T(128)S(1)} all-reduce(f32[128]{0:T(128)S(1)} %dynamic-update-slice), channel_id=2, replica_groups=mesh['bump'=4,'nx'=2,'ny'=4] {'nx','ny'}, use_global_device_ids=true, to_apply=%add | all-reduce | flops 128 | bytes 1024
  (134 shorter events, 21.1 us)
Async XLA Ops:
  7.2 19.2 %copy-start.28 = (f32[16]{0:T(128)S(1)}, f32[16]{0:T(128)}, u32[]{:S(2)}) copy-start(f32[16]{0:T(128)} %param.13) | copy-start | bytes 196
  7.2 19.2 %copy-start.27 = (s32[16]{0:T(128)S(1)}, s32[16]{0:T(128)}, u32[]{:S(2)}) copy-start(s32[16]{0:T(128)} %param.12) | copy-start | bytes 196
  7.2 64.7 %all-gather.3.cloned.1.call-start = ((), (), s32[]{:S(2)}) async-start(), calls=%async_computation | async-start | bytes 10485760 | tf_op jit(solution)/shard_map/all_gather | solution.py:50
  10.8 81.4 %collective-permute-start.1 = (f32[17,2]{1,0:T(8,128)S(1)}, f32[17,2]{1,0:T(8,128)S(1)}, u32[]{:S(2)}, u32[]{:S(2)}) collective-permute-start(f32[17,2]{1,0:T(8,128)S(1)} %broadcast_in_dim.178), channel_id=1, source_target_pairs={{1,0},{2,1},{3,2},{4,3},{5,4},{6,5},{7,6},{0,7},{9,8},{10,9},{11,1... | collective-permute-start | bytes 416 | tf_op jit(solution)/shard_map/ppermute | solution.py:15
  16.9 75.4 %collective-permute-start = (f32[17,2]{1,0:T(8,128)S(1)}, f32[17,2]{1,0:T(8,128)S(1)}, u32[]{:S(2)}, u32[]{:S(2)}) collective-permute-start(f32[17,2]{1,0:T(8,128)S(1)} %broadcast_in_dim.175), channel_id=1, source_target_pairs={{0,1},{1,2},{2,3},{3,4},{4,5},{5,6},{6,7},{7,0},{8,9},{9,10},{10,1... | collective-permute-start | bytes 416 | tf_op jit(solution)/shard_map/ppermute | solution.py:14
  99.6 6.4 %collective-permute-start.2 = (f32[17,2]{1,0:T(8,128)S(1)}, f32[17,2]{1,0:T(8,128)S(1)}, u32[]{:S(2)}, u32[]{:S(2)}) collective-permute-start(f32[17,2]{1,0:T(8,128)S(1)} %get-tuple-element.56), channel_id=1, source_target_pairs={{0,1},{1,2},{2,3},{3,4},{4,5},{5,6},{6,7},{7,0},{8,9},{9,10},{10,1... | collective-permute-start | bytes 416 | tf_op jit(solution)/shard_map/ppermute | solution.py:14
  101.1 4.9 %collective-permute-start.3 = (f32[17,2]{1,0:T(8,128)S(1)}, f32[17,2]{1,0:T(8,128)S(1)}, u32[]{:S(2)}, u32[]{:S(2)}) collective-permute-start(f32[17,2]{1,0:T(8,128)S(1)} %get-tuple-element.57), channel_id=1, source_target_pairs={{1,0},{2,1},{3,2},{4,3},{5,4},{6,5},{7,6},{0,7},{9,8},{10,9},{11,1... | collective-permute-start | bytes 416 | tf_op jit(solution)/shard_map/ppermute | solution.py:15
  106.6 15.4 %copy-start.25 = (pred[128]{0:T(512)(128)(4,1)S(1)}, pred[128]{0:T(512)(128)(4,1)}, u32[]{:S(2)}) copy-start(pred[128]{0:T(512)(128)(4,1)} %get-tuple-element.73) | copy-start | bytes 388
  117.3 6.8 %collective-permute-start.4 = (f32[17,2]{1,0:T(8,128)}, f32[17,2]{1,0:T(8,128)}, u32[]{:S(2)}, u32[]{:S(2)}) collective-permute-start(f32[17,2]{1,0:T(8,128)} %get-tuple-element.54), channel_id=1, source_target_pairs={{0,1},{1,2},{2,3},{3,4},{4,5},{5,6},{6,7},{7,0},{8,9},{9,10},{10,1... | collective-permute-start | bytes 416 | tf_op jit(solution)/shard_map/ppermute | solution.py:14
  117.6 6.5 %collective-permute-start.5 = (f32[17,2]{1,0:T(8,128)S(1)}, f32[17,2]{1,0:T(8,128)}, u32[]{:S(2)}, u32[]{:S(2)}) collective-permute-start(f32[17,2]{1,0:T(8,128)S(1)} %get-tuple-element.55), channel_id=1, source_target_pairs={{1,0},{2,1},{3,2},{4,3},{5,4},{6,5},{7,6},{0,7},{9,8},{10,9},{11,1... | collective-permute-start | bytes 416 | tf_op jit(solution)/shard_map/ppermute | solution.py:15
  132.3 6.4 %collective-permute-start.6 = (f32[17,2]{1,0:T(8,128)S(1)}, f32[17,2]{1,0:T(8,128)S(1)}, u32[]{:S(2)}, u32[]{:S(2)}) collective-permute-start(f32[17,2]{1,0:T(8,128)S(1)} %get-tuple-element.52), channel_id=1, source_target_pairs={{0,1},{1,2},{2,3},{3,4},{4,5},{5,6},{6,7},{7,0},{8,9},{9,10},{10,1... | collective-permute-start | bytes 416 | tf_op jit(solution)/shard_map/ppermute | solution.py:14
  133.1 5.6 %collective-permute-start.7 = (f32[17,2]{1,0:T(8,128)S(1)}, f32[17,2]{1,0:T(8,128)S(1)}, u32[]{:S(2)}, u32[]{:S(2)}) collective-permute-start(f32[17,2]{1,0:T(8,128)S(1)} %get-tuple-element.53), channel_id=1, source_target_pairs={{1,0},{2,1},{3,2},{4,3},{5,4},{6,5},{7,6},{0,7},{9,8},{10,9},{11,1... | collective-permute-start | bytes 416 | tf_op jit(solution)/shard_map/ppermute | solution.py:15
  150.0 6.7 %collective-permute-start.8 = (f32[17,2]{1,0:T(8,128)}, f32[17,2]{1,0:T(8,128)}, u32[]{:S(2)}, u32[]{:S(2)}) collective-permute-start(f32[17,2]{1,0:T(8,128)} %get-tuple-element.50), channel_id=1, source_target_pairs={{0,1},{1,2},{2,3},{3,4},{4,5},{5,6},{6,7},{7,0},{8,9},{9,10},{10,1... | collective-permute-start | bytes 416 | tf_op jit(solution)/shard_map/ppermute | solution.py:14
  150.8 5.9 %collective-permute-start.9 = (f32[17,2]{1,0:T(8,128)S(1)}, f32[17,2]{1,0:T(8,128)}, u32[]{:S(2)}, u32[]{:S(2)}) collective-permute-start(f32[17,2]{1,0:T(8,128)S(1)} %get-tuple-element.51), channel_id=1, source_target_pairs={{1,0},{2,1},{3,2},{4,3},{5,4},{6,5},{7,6},{0,7},{9,8},{10,9},{11,1... | collective-permute-start | bytes 416 | tf_op jit(solution)/shard_map/ppermute | solution.py:15
  156.7 13.1 %copy-start.7 = (f32[1,1,32768]{2,1,0:T(1,128)S(1)}, f32[1,1,32768]{2,1,0:T(1,128)}, u32[]{:S(2)}) copy-start(f32[1,1,32768]{2,1,0:T(1,128)} %get-tuple-element.37) | copy-start | bytes 393220
  156.7 13.1 %copy-start.8 = (f32[1,1,32768]{2,1,0:T(1,128)S(1)}, f32[1,1,32768]{2,1,0:T(1,128)}, u32[]{:S(2)}) copy-start(f32[1,1,32768]{2,1,0:T(1,128)} %get-tuple-element.38) | copy-start | bytes 393220
  156.7 13.1 %copy-start.9 = (f32[1,1,32768]{2,1,0:T(1,128)S(1)}, f32[1,1,32768]{2,1,0:T(1,128)}, u32[]{:S(2)}) copy-start(f32[1,1,32768]{2,1,0:T(1,128)} %get-tuple-element.39) | copy-start | bytes 393220
  156.7 13.1 %copy-start.10 = (f32[1,1,32768]{2,1,0:T(1,128)S(1)}, f32[1,1,32768]{2,1,0:T(1,128)}, u32[]{:S(2)}) copy-start(f32[1,1,32768]{2,1,0:T(1,128)} %get-tuple-element.9) | copy-start | bytes 393220
  156.7 13.1 %copy-start.11 = (f32[1,1,32768]{2,1,0:T(1,128)S(1)}, f32[1,1,32768]{2,1,0:T(1,128)}, u32[]{:S(2)}) copy-start(f32[1,1,32768]{2,1,0:T(1,128)} %get-tuple-element.10) | copy-start | bytes 393220
  156.7 13.1 %copy-start.16 = (pred[32768]{0:T(1024)(128)(4,1)S(1)}, pred[32768]{0:T(1024)(128)(4,1)}, u32[]{:S(2)}) copy-start(pred[32768]{0:T(1024)(128)(4,1)} %eq.297) | copy-start | bytes 98308
  156.7 13.1 %copy-start.17 = (pred[32768]{0:T(1024)(128)(4,1)S(1)}, pred[32768]{0:T(1024)(128)(4,1)}, u32[]{:S(2)}) copy-start(pred[32768]{0:T(1024)(128)(4,1)} %eq.264) | copy-start | bytes 98308
  156.8 13.1 %copy-start.24 = (f32[17]{0:T(128)S(1)}, f32[17]{0:T(128)}, u32[]{:S(2)}) copy-start(f32[17]{0:T(128)} %get-tuple-element.82) | copy-start | bytes 208
  163.4 6.4 %collective-permute-start.10 = (f32[17,2]{1,0:T(8,128)S(1)}, f32[17,2]{1,0:T(8,128)S(1)}, u32[]{:S(2)}, u32[]{:S(2)}) collective-permute-start(f32[17,2]{1,0:T(8,128)S(1)} %get-tuple-element.48), channel_id=1, source_target_pairs={{0,1},{1,2},{2,3},{3,4},{4,5},{5,6},{6,7},{7,0},{8,9},{9,10},{10,1... | collective-permute-start | bytes 416 | tf_op jit(solution)/shard_map/ppermute | solution.py:14
  164.3 5.5 %collective-permute-start.11 = (f32[17,2]{1,0:T(8,128)S(1)}, f32[17,2]{1,0:T(8,128)S(1)}, u32[]{:S(2)}, u32[]{:S(2)}) collective-permute-start(f32[17,2]{1,0:T(8,128)S(1)} %get-tuple-element.49), channel_id=1, source_target_pairs={{1,0},{2,1},{3,2},{4,3},{5,4},{6,5},{7,6},{0,7},{9,8},{10,9},{11,1... | collective-permute-start | bytes 416 | tf_op jit(solution)/shard_map/ppermute | solution.py:15
  169.9 12.1 %copy-start.3 = (f32[1,1,32768]{2,1,0:T(1,128)S(1)}, f32[1,1,32768]{2,1,0:T(1,128)}, u32[]{:S(2)}) copy-start(f32[1,1,32768]{2,1,0:T(1,128)} %get-tuple-element.40) | copy-start | bytes 393220
  169.9 12.1 %copy-start.4 = (f32[1,1,32768]{2,1,0:T(1,128)S(1)}, f32[1,1,32768]{2,1,0:T(1,128)}, u32[]{:S(2)}) copy-start(f32[1,1,32768]{2,1,0:T(1,128)} %get-tuple-element.41) | copy-start | bytes 393220
  169.9 12.1 %copy-start.5 = (f32[1,1,32768]{2,1,0:T(1,128)S(1)}, f32[1,1,32768]{2,1,0:T(1,128)}, u32[]{:S(2)}) copy-start(f32[1,1,32768]{2,1,0:T(1,128)} %get-tuple-element.7) | copy-start | bytes 393220
  175.4 6.5 %collective-permute-start.12 = (f32[17,2]{1,0:T(8,128)S(1)}, f32[17,2]{1,0:T(8,128)S(1)}, u32[]{:S(2)}, u32[]{:S(2)}) collective-permute-start(f32[17,2]{1,0:T(8,128)S(1)} %get-tuple-element.46), channel_id=1, source_target_pairs={{0,1},{1,2},{2,3},{3,4},{4,5},{5,6},{6,7},{7,0},{8,9},{9,10},{10,1... | collective-permute-start | bytes 416 | tf_op jit(solution)/shard_map/ppermute | solution.py:14
  176.3 5.7 %collective-permute-start.13 = (f32[17,2]{1,0:T(8,128)S(1)}, f32[17,2]{1,0:T(8,128)S(1)}, u32[]{:S(2)}, u32[]{:S(2)}) collective-permute-start(f32[17,2]{1,0:T(8,128)S(1)} %get-tuple-element.47), channel_id=1, source_target_pairs={{1,0},{2,1},{3,2},{4,3},{5,4},{6,5},{7,6},{0,7},{9,8},{10,9},{11,1... | collective-permute-start | bytes 416 | tf_op jit(solution)/shard_map/ppermute | solution.py:15
  187.6 6.4 %collective-permute-start.14 = (f32[17,2]{1,0:T(8,128)S(1)}, f32[17,2]{1,0:T(8,128)S(1)}, u32[]{:S(2)}, u32[]{:S(2)}) collective-permute-start(f32[17,2]{1,0:T(8,128)S(1)} %get-tuple-element.44), channel_id=1, source_target_pairs={{0,1},{1,2},{2,3},{3,4},{4,5},{5,6},{6,7},{7,0},{8,9},{9,10},{10,1... | collective-permute-start | bytes 416 | tf_op jit(solution)/shard_map/ppermute | solution.py:14
  188.5 5.5 %collective-permute-start.15 = (f32[17,2]{1,0:T(8,128)S(1)}, f32[17,2]{1,0:T(8,128)S(1)}, u32[]{:S(2)}, u32[]{:S(2)}) collective-permute-start(f32[17,2]{1,0:T(8,128)S(1)} %get-tuple-element.45), channel_id=1, source_target_pairs={{1,0},{2,1},{3,2},{4,3},{5,4},{6,5},{7,6},{0,7},{9,8},{10,9},{11,1... | collective-permute-start | bytes 416 | tf_op jit(solution)/shard_map/ppermute | solution.py:15
  199.5 24.2 %copy-start.29 = (f32[16]{0:T(128)S(1)}, f32[16]{0:T(128)}, u32[]{:S(2)}) copy-start(f32[16]{0:T(128)} %param.13) | copy-start | bytes 196
  (16 other events, 128.8 us)
Sparse Core Ops, SparseCore 0:
  10.9 60.9 all-gather.2
